TPU v7x, 32 devices: a whole 2x2x4 slice. The times are simulated.
32 devices in a mesh: section: 2 (over y), dp: 16 (over z, x, core).
Axes of the slice: x: 2, y: 2, z: 4, core: 2. Of those that a mesh axis runs over, the one named last changes fastest.
Arguments:
- activations: bfloat16 [2, 4, 16, 14336], P('section', None, 'dp'), may hold values from -6 to 6
- out_grads: bfloat16 [2, 4, 16, 4096], P('section', None, 'dp'), may hold values from -6 to 6
- basis_in: bfloat16 [2, 14336, 1024], P('section', 'dp'), may hold values from -0.046875 to 0.046875
- basis_out: bfloat16 [2, 4096, 1024], P('section', 'dp'), may hold values from -0.09375 to 0.09375
- eigen_values: float32 [2, 1024, 1024], P('section', 'dp'), may hold values from 0.02 to 2
- query_proj: bfloat16 [2, 8, 1024, 1024], P('section', None, 'dp'), may hold values from -0.046875 to 0.046875
- lengths: int32 [4], replicated, may hold values from 4 to 16
- seq_rows: int32 [4], replicated, may hold values from 0 to 127
- prior_table: float32 [128, 8], P('dp'), may hold values from -6 to 6
Outputs:
- influence: float32 [2, 128, 8], P('section', 'dp')
All inputs are finite; a program needn't handle non-finite values.
Results may differ from a plain program's by a relative error of at most 0.01.
Values may be sent and summed in bfloat16 or wider, within the bound.
No kernel may reach another device: no remote copies, remote signals or barrier semaphores. Data moves between devices by JAX's collectives and lax.ppermute only.
A program may use at most 64 MiB of HBM per device.

v0:
```python
import jax
import jax.numpy as jnp
from jax import lax
from jax.sharding import PartitionSpec as P

DAMPING = 0.01


def entering(value, axis, join, neutral):
    count, mine = (lax.axis_size(axis), lax.axis_index(axis))
    pieces = lax.all_gather(value, axis)
    running = jnp.full_like(value, 0) + jnp.asarray(neutral, value.dtype)

    def step(position, running):
        longer = join(running, pieces[position])
        return jnp.where(position < mine, longer, running)

    return lax.fori_loop(0, count - 1, step, running)


def add_pair(earlier, latter):
    return earlier + latter


def per_device(
    activations,
    out_grads,
    basis_in,
    basis_out,
    eigen_values,
    query_proj,
    lengths,
    seq_rows,
    prior_table,
):
    micro = activations.shape[1]
    cols_acts, cols_grads = (
        lax.all_to_all(activations[0], "dp", split_axis=2, concat_axis=1, tiled=True),
        lax.all_to_all(out_grads[0], "dp", split_axis=2, concat_axis=1, tiled=True),
    )
    slots = cols_acts.shape[1]
    rank_size = basis_in.shape[2]
    act_part = jnp.dot(
        cols_acts.reshape(micro * slots, cols_acts.shape[2]),
        basis_in[0],
        preferred_element_type=jnp.float32,
    )
    grad_part = jnp.dot(
        cols_grads.reshape(micro * slots, cols_grads.shape[2]),
        basis_out[0],
        preferred_element_type=jnp.float32,
    )
    grad_share = lax.psum_scatter(grad_part, "dp", scatter_dimension=1, tiled=True).astype(
        jnp.bfloat16
    )
    act_proj = lax.psum(act_part, "dp").astype(jnp.bfloat16)
    block_rows = grad_share.shape[1]
    position = jnp.arange(slots, dtype=jnp.int32)
    live_mask = (position[None, :] < lengths[:, None]).reshape(micro * slots, 1)
    grad_share = jnp.where(live_mask, grad_share, jnp.zeros_like(grad_share))
    inverse_len = 1.0 / lengths.astype(jnp.float32)
    seq_block = (
        jnp.einsum(
            "mti,mtj->mij",
            grad_share.reshape(micro, slots, block_rows),
            act_proj.reshape(micro, slots, rank_size),
            preferred_element_type=jnp.float32,
        )
        * inverse_len[:, None, None]
    )
    precond = (query_proj[0].astype(jnp.float32) / (eigen_values[0][None] + DAMPING)).astype(
        jnp.bfloat16
    )
    partial_value = jnp.einsum(
        "mij,qij->mq", seq_block, precond.astype(jnp.float32), precision=lax.Precision.HIGHEST
    )
    table_rows = prior_table.shape[0]
    first_row = lax.axis_index("dp") * table_rows
    summed = lax.psum(partial_value, "dp")
    before = entering(summed, "section", add_pair, jnp.zeros_like(summed))
    owner_mask = (
        seq_rows[None, :] == (first_row + jnp.arange(table_rows, dtype=jnp.int32))[:, None]
    ).astype(jnp.float32)
    result = prior_table + jnp.dot(owner_mask, before + summed, precision=lax.Precision.HIGHEST)
    return result[None]


def solution(mesh):
    return jax.shard_map(
        per_device,
        mesh=mesh,
        in_specs=(
            P("section", None, "dp", None),
            P("section", None, "dp", None),
            P("section", "dp", None),
            P("section", "dp", None),
            P("section", "dp", None),
            P("section", None, "dp", None),
            P(),
            P(),
            P("dp", None),
        ),
        out_specs=P("section", "dp", None),
        check_vma=False,
    )
```

profile of v0, /device:TPU:0, one launch (start us, length us, event | category | flops | bytes accessed | tf_op | source)
XLA Modules:
  0.0 303.3 jit_solution(3628222360008374152)
XLA Ops:
  6.5 0.0 copy-start
  6.5 5.0 %copy.14 = bf16[4,1,4096]{0,1,2:T(2,128)(2,1)} copy(bf16[4,1,4096]{2,0,1:T(4,128)(2,1)} %bitcast.47) | data formatting | bytes 65536 | tf_op jit(solution)/shard_map/squeeze | solution.py:39
  11.5 0.5 broadcast.36
  12.1 23.5 %reduce = bf16[4096,4]{1,0:T(8,128)(2,1)S(1)} reduce(bf16[4096,1,4]{2,1,0:T(2,128)(2,1)} %bitcast.42, bf16[]{:T(256)} %broadcast.36), dimensions={1}, to_apply=%bitcast.32.reduce_sub_computation | reduce | bytes 65538
  35.5 2.6 reshape.67
  38.1 7.4 %all-to-all-start = ((bf16[16,2,512]{2,1,0:T(2,128)(2,1)}), bf16[16,2,512]{2,1,0:T(2,128)(2,1)S(1)}, u32[]{:S(2)}, u32[]{:S(2)}) async-start(bf16[16,2,512]{2,1,0:T(2,128)(2,1)} %reshape.67), calls=%async_computation | async-start | bytes 65536 | tf_op jit(solution)/shard_map/all_to_all | solution.py:39
  45.5 0.0 copy-done.7
  45.6 0.1 iota_compare_fusion
  45.6 0.5 convert_divide_fusion.1
  46.2 0.0 copy-done.3
  46.2 11.6 %copy.16 = bf16[4,1,14336]{0,1,2:T(2,128)(2,1)} copy(bf16[4,1,14336]{2,0,1:T(4,128)(2,1)S(1)} %bitcast.45) | data formatting | bytes 229376 | tf_op jit(solution)/shard_map/squeeze | solution.py:38
  57.7 79.8 %reduce.1 = bf16[14336,4]{1,0:T(8,128)(2,1)} reduce(bf16[14336,1,4]{2,1,0:T(2,128)(2,1)} %bitcast.41, bf16[]{:T(256)} %broadcast.36), dimensions={1}, to_apply=%bitcast.34.reduce_sub_computation | reduce | bytes 229378
  137.6 8.3 %reshape.69 = bf16[16,2,1792]{2,1,0:T(2,128)(2,1)} reshape(bf16[14336,4]{1,0:T(8,128)(2,1)} %reduce.1) | data formatting | bytes 229376
  145.8 0.6 lt.31
  146.4 0.0 copy-done.2
  146.5 1.5 fusion
  148.0 0.5 iota_add_fusion
  148.6 0.0 all-to-all-done
  148.6 6.0 %all-to-all-start.1 = ((bf16[16,2,1792]{2,1,0:T(2,128)(2,1)}), bf16[16,2,1792]{2,1,0:T(2,128)(2,1)S(1)}, u32[]{:S(2)}, u32[]{:S(2)}) async-start(bf16[16,2,1792]{2,1,0:T(2,128)(2,1)} %reshape.69), calls=%async_computation.1 | async-start | bytes 229376 | tf_op jit(solution)/shard_map/all_to_all | solution.py:38
  154.6 0.0 copy-start.1
  154.6 0.0 reduce-scatter.4.cloned.1.call-start
  154.6 4.5 %reshape.68 = bf16[4096,1,4]{2,1,0:T(2,128)(2,1)} reshape(bf16[16,2,512]{2,1,0:T(2,128)(2,1)S(1)} %all-to-all-done) | data formatting | bytes 65536
  159.2 4.5 %copy.15 = bf16[4,1,4096]{2,0,1:T(4,128)(2,1)S(1)} copy(bf16[4,1,4096]{0,1,2:T(2,128)(2,1)} %bitcast.43) | data formatting | bytes 65536 | tf_op jit(solution)/shard_map/all_to_all | solution.py:39
  163.7 0.6 reshape.47
  164.3 0.0 copy-done.1
  164.4 1.9 convolution_bitcast_fusion
  166.2 0.0 reduce-scatter.4.cloned.1.call-update
  166.3 0.0 all-to-all-done.1
  166.3 11.5 %reshape.70 = bf16[14336,1,4]{2,1,0:T(2,128)(2,1)} reshape(bf16[16,2,1792]{2,1,0:T(2,128)(2,1)S(1)} %all-to-all-done.1) | data formatting | bytes 229376
  177.8 13.9 %copy.17 = bf16[4,1,14336]{2,0,1:T(4,128)(2,1)S(1)} copy(bf16[4,1,14336]{0,1,2:T(2,128)(2,1)} %bitcast.40) | data formatting | bytes 229376 | tf_op jit(solution)/shard_map/all_to_all | solution.py:38
  191.7 0.0 copy-start.5
  191.8 0.1 reshape.49
  191.9 0.4 fusion.1
  192.3 0.0 copy-start.6
  192.3 0.0 copy-start.8
  192.3 0.0 copy-start.9
  192.3 64.6 %all-reduce.1 = bf16[64,1024]{1,0:T(8,128)(2,1)S(1)} all-reduce(f32[64,1024]{1,0:T(8,128)S(1)} %fusion.1), channel_id=1, replica_groups=mesh['section'=2,'dp'=16] {'dp'}, use_global_device_ids=true, to_apply=%region_1.0 | all-reduce | flops 65536 | bytes 393216 | tf_op jit(solution)/shard_map/psum | solution.py:56
  256.9 0.0 reduce-scatter.4.cloned.1.call-done
  257.0 0.8 copy.21
  257.8 0.0 copy-done.5
  257.8 0.1 convert_select_fusion
  257.9 0.0 copy-done.4
  257.9 0.3 convolution_multiply_fusion
  258.3 3.5 %convolution_bitcast_fusion.1 = f32[4,8]{1,0:T(4,128)S(1)} fusion(bf16[8,64,1024]{2,1,0:T(8,128)(2,1)S(1)} %fusion, f32[4,64,1024]{2,1,0:T(8,128)S(1)} %convolution_multiply_fusion), kind=kOutput, calls=%fused_computation.8 | convolution fusion | flops 25165824 | bytes 2097280 | tf_op jit(solution)/shard_map/mij,qij->mq/dot_general | solution.py:74
  261.8 29.5 %psum.15 = f32[4,8]{1,0:T(4,128)S(1)} all-reduce(f32[4,8]{1,0:T(4,128)S(1)} %convolution_bitcast_fusion.1), channel_id=1, replica_groups=mesh['section'=2,'dp'=16] {'dp'}, use_global_device_ids=true, to_apply=%region_2.3 | all-reduce | flops 32 | bytes 256 | tf_op jit(solution)/shard_map/psum | solution.py:79
  291.3 4.4 %all-gather.1 = f32[2,4,8]{2,1,0:T(4,128)S(1)} all-gather(f32[1,4,8]{2,1,0:T(4,128)S(1)} %bitcast.49), channel_id=2, replica_groups=mesh['section'=2,'dp'=16] {'section'}, dimensions={0}, use_global_device_ids=true | all-gather | bytes 384 | tf_op jit(solution)/shard_map/all_gather | solution.py:11
  295.6 0.0 copy-done.8
  295.6 0.8 fusion.3
  (8 shorter events, 0.0 us)
Async XLA Ops:
  6.5 185.3 %copy-start = (bf16[1,896,1024]{2,1,0:T(8,128)(2,1)S(1)}, bf16[1,896,1024]{2,1,0:T(8,128)(2,1)}, u32[]{:S(2)}) copy-start(bf16[1,896,1024]{2,1,0:T(8,128)(2,1)} %param.11) | copy-start | bytes 5505028
  12.1 33.5 %copy-start.7 = (s32[4]{0:T(128)S(1)}, s32[4]{0:T(128)}, u32[]{:S(2)}) copy-start(s32[4]{0:T(128)} %param.15) | copy-start | bytes 52
  12.1 34.1 %copy-start.3 = (bf16[1,4,1,14336]{3,1,2,0:T(4,128)(2,1)S(1)}, bf16[1,4,1,14336]{3,1,2,0:T(4,128)(2,1)}, u32[]{:S(2)}) copy-start(bf16[1,4,1,14336]{3,1,2,0:T(4,128)(2,1)} %param.9) | copy-start | bytes 344068
  38.1 110.4 %all-to-all-start = ((bf16[16,2,512]{2,1,0:T(2,128)(2,1)}), bf16[16,2,512]{2,1,0:T(2,128)(2,1)S(1)}, u32[]{:S(2)}, u32[]{:S(2)}) async-start(bf16[16,2,512]{2,1,0:T(2,128)(2,1)} %reshape.67), calls=%async_computation | async-start | bytes 65536 | tf_op jit(solution)/shard_map/all_to_all | solution.py:39
  137.6 8.9 %copy-start.2 = (f32[1,64,1024]{2,1,0:T(8,128)S(1)}, f32[1,64,1024]{2,1,0:T(8,128)}, u32[]{:S(2)}) copy-start(f32[1,64,1024]{2,1,0:T(8,128)} %param.13) | copy-start | bytes 786436
  148.6 17.7 %all-to-all-start.1 = ((bf16[16,2,1792]{2,1,0:T(2,128)(2,1)}), bf16[16,2,1792]{2,1,0:T(2,128)(2,1)S(1)}, u32[]{:S(2)}, u32[]{:S(2)}) async-start(bf16[16,2,1792]{2,1,0:T(2,128)(2,1)} %reshape.69), calls=%async_computation.1 | async-start | bytes 229376 | tf_op jit(solution)/shard_map/all_to_all | solution.py:38
  154.6 9.8 %copy-start.1 = (bf16[1,256,1024]{2,1,0:T(8,128)(2,1)S(1)}, bf16[1,256,1024]{2,1,0:T(8,128)(2,1)}, u32[]{:S(2)}) copy-start(bf16[1,256,1024]{2,1,0:T(8,128)(2,1)} %param.12) | copy-start | bytes 1572868
  154.6 102.4 %reduce-scatter.4.cloned.1.call-start = ((), (), s32[]{:S(2)}) async-start(), calls=%async_computation.3 | async-start | bytes 557056
  191.7 66.1 %copy-start.5 = (pred[64]{0:T(512)(128)(4,1)S(1)}, pred[64]{0:T(512)(128)(4,1)}, u32[]{:S(2)}) copy-start(pred[64]{0:T(512)(128)(4,1)} %lt.31) | copy-start | bytes 196
  191.7 66.1 %copy-start.4 = (f32[4]{0:T(128)S(1)}, f32[4]{0:T(128)}, u32[]{:S(2)}) copy-start(f32[4]{0:T(128)} %convert_divide_fusion.1) | copy-start | bytes 52
  192.3 103.3 %copy-start.6 = (f32[8,8]{1,0:T(8,128)S(1)}, f32[8,8]{1,0:T(8,128)}, u32[]{:S(2)}) copy-start(f32[8,8]{1,0:T(8,128)} %param.17) | copy-start | bytes 772
  192.3 103.3 %copy-start.8 = (s32[4]{0:T(128)S(1)}, s32[4]{0:T(128)}, u32[]{:S(2)}) copy-start(s32[4]{0:T(128)} %param.16) | copy-start | bytes 52
  192.3 103.3 %copy-start.9 = (s32[8]{0:T(128)S(1)}, s32[8]{0:T(128)}, u32[]{:S(2)}) copy-start(s32[8]{0:T(128)} %iota_add_fusion) | copy-start | bytes 100
Sparse Core Ops, SparseCore 0:
  166.4 57.5 reduce-scatter.3
where the time goes:
time: 304 us; the launch traced here: 303 us
  other arithmetic  106 us (35%)
  blocking collectives  98.4 us (32%)
  local copies, waits for them, and re-layouts  64.7 us (21%)
  between operations  13.6 us (4%)
  starting transfers between devices  13.4 us (4%)
  matrix products  6.96 us (2%)
    unnamed x2, other arithmetic  103 us
    psum x1, blocking collectives, per_device(): act_proj = lax.psum(act_part, 'dp').astype(jnp.bfloat16)  64.6 us
    psum x1, blocking collectives, per_device(): summed = lax.psum(partial_value, 'dp')  29.5 us
    unnamed x26, local copies, waits for them, and re-layouts  28.3 us
    all_to_all x1, local copies, waits for them, and re-layouts, per_device(): lax.all_to_all(activations[0], 'dp', split_axis=2, concat_axis=1, tiled=T...  13.9 us
    squeeze x1, local copies, waits for them, and re-layouts, per_device(): activations[0]  11.6 us
    all_to_all x1, starting transfers between devices, per_device(): lax.all_to_all(out_grads[0], 'dp', split_axis=2, concat_axis=1, tiled=True)  7.39 us
  transfers between devices with their start and end apart: 3, of which 0 were waited for; matrix products, arithmetic and copies ran while one was open for 46% of the time, Pallas kernels for 0%

commit v1 on v0

--- a/solution.py
+++ b/solution.py
@@ -34,8 +34,17 @@
     prior_table,
 ):
     micro = activations.shape[1]
+    edges_start = lambda s0, dim_k, at_axis: jnp.concatenate(
+        lax.all_to_all(
+            jnp.stack(jnp.split(s0, lax.psum(1, "dp"), dim_k), axis=0),
+            "dp",
+            concat_axis=0,
+            split_axis=0,
+        ),
+        axis=at_axis,
+    )
     cols_acts, cols_grads = (
-        lax.all_to_all(activations[0], "dp", split_axis=2, concat_axis=1, tiled=True),
+        edges_start(activations[0], 2, 1),
         lax.all_to_all(out_grads[0], "dp", split_axis=2, concat_axis=1, tiled=True),
     )
     slots = cols_acts.shape[1]

time: 304 us -> 188 us (0.62)
  other arithmetic: 106 us -> 26.2 us
  local copies, waits for them, and re-layouts: 64.7 us -> 28.8 us
    unnamed x2 -> x1, other arithmetic: 103 us -> 23.5 us
    all_to_all x1 -> x0, local copies, waits for them, and re-layouts: 13.9 us -> none  [per_device(): lax.all_to_all(activations[0], 'dp', split_axis=2, concat_axis=1, tiled=T...]
    squeeze x1 -> x0, local copies, waits for them, and re-layouts: 11.6 us -> none  [per_device(): activations[0]]
    unnamed x26 -> x39, local copies, waits for them, and re-layouts: 28.3 us -> 17.5 us
  transfers between devices with their start and end apart: 3 -> 3, of which waited for: 0 -> 0; matrix products, arithmetic and copies ran while one was open for 46% -> 13% of each run, Pallas kernels for 0% -> 0%
where the time goes in v1:
time: 188 us
  blocking collectives  98.5 us (52%)
  local copies, waits for them, and re-layouts  28.8 us (15%)
  other arithmetic  26.2 us (14%)
  between operations  13.6 us (7%)
  starting transfers between devices  13.4 us (7%)
  matrix products  6.99 us (4%)
    psum x1, blocking collectives, per_device(): act_proj = lax.psum(act_part, 'dp').astype(jnp.bfloat16)  64.7 us
    psum x1, blocking collectives, per_device(): summed = lax.psum(partial_value, 'dp')  29.5 us
    unnamed x1, other arithmetic  23.5 us
    unnamed x39, local copies, waits for them, and re-layouts  17.5 us
    all_to_all x1, starting transfers between devices, per_device(): lax.all_to_all(out_grads[0], 'dp', split_axis=2, concat_axis=1, tiled=True)  7.39 us
    all_to_all x1, starting transfers between devices, per_device(): lax.all_to_all(jnp.stack(jnp.split(s0, lax.psum(1, 'dp'), dim_k), axis=0)...  6.01 us
    squeeze x1, local copies, waits for them, and re-layouts, per_device(): out_grads[0]  5 us
    all_to_all x1, local copies, waits for them, and re-layouts, per_device(): lax.all_to_all(out_grads[0], 'dp', split_axis=2, concat_axis=1, tiled=True)  4.53 us
  transfers between devices with their start and end apart: 3, of which 0 were waited for; matrix products, arithmetic and copies ran while one was open for 13% of the time, Pallas kernels for 0%

profile of v1, /device:TPU:0, one launch (start us, length us, event | category | flops | bytes accessed | tf_op | source)
XLA Modules:
  0.0 187.7 jit_solution(15974958571506428424)
XLA Ops:
  6.5 5.0 %copy.34 = bf16[4,1,4096]{0,1,2:T(2,128)(2,1)} copy(bf16[4,1,4096]{2,0,1:T(4,128)(2,1)} %bitcast.124) | data formatting | bytes 65536 | tf_op jit(solution)/shard_map/squeeze | solution.py:48
  11.5 0.5 broadcast.36
  12.1 23.5 %reduce = bf16[4096,4]{1,0:T(8,128)(2,1)S(1)} reduce(bf16[4096,1,4]{2,1,0:T(2,128)(2,1)} %bitcast.102, bf16[]{:T(256)} %broadcast.36), dimensions={1}, to_apply=%bitcast.96.reduce_sub_computation | reduce | bytes 65538
  35.6 2.6 %reshape.63 = bf16[16,2,512]{2,1,0:T(2,128)(2,1)} reshape(bf16[4096,4]{1,0:T(8,128)(2,1)S(1)} %reduce) | data formatting | bytes 65536
  38.1 7.4 %all-to-all-start = ((bf16[16,2,512]{2,1,0:T(2,128)(2,1)}), bf16[16,2,512]{2,1,0:T(2,128)(2,1)S(1)}, u32[]{:S(2)}, u32[]{:S(2)}) async-start(bf16[16,2,512]{2,1,0:T(2,128)(2,1)} %reshape.63), calls=%async_computation | async-start | bytes 65536 | tf_op jit(solution)/shard_map/all_to_all | solution.py:48
  45.5 0.1 iota_compare_fusion
  45.6 0.5 convert_divide_fusion.1
  46.1 0.6 constant_dynamic-update-slice_fusion.15
  46.7 0.6 constant_dynamic-update-slice_fusion.14
  47.3 0.6 constant_dynamic-update-slice_fusion.13
  47.9 0.6 constant_dynamic-update-slice_fusion.12
  48.5 0.6 constant_dynamic-update-slice_fusion.11
  49.1 0.6 constant_dynamic-update-slice_fusion.10
  49.7 0.6 constant_dynamic-update-slice_fusion.9
  50.3 0.6 constant_dynamic-update-slice_fusion.8
  50.9 0.6 constant_dynamic-update-slice_fusion.7
  51.5 0.6 constant_dynamic-update-slice_fusion.6
  52.1 0.6 constant_dynamic-update-slice_fusion.5
  52.7 0.6 constant_dynamic-update-slice_fusion.4
  53.3 0.6 constant_dynamic-update-slice_fusion.3
  53.9 0.6 constant_dynamic-update-slice_fusion.2
  54.5 0.6 constant_dynamic-update-slice_fusion.1
  55.1 0.6 constant_dynamic-update-slice_fusion
  55.7 0.6 lt.31
  56.3 1.5 fusion
  57.9 0.5 iota_add_fusion
  58.4 6.0 %all-to-all-start.1 = ((bf16[16,4,1,896]{3,1,2,0:T(4,128)(2,1)}), bf16[16,4,1,896]{3,1,2,0:T(4,128)(2,1)S(1)}, u32[]{:S(2)}, u32[]{:S(2)}) async-start(bf16[16,4,1,896]{3,1,2,0:T(4,128)(2,1)} %constant_dynamic-update-slice_fusion), calls=%async_computation.1 | async-start | bytes 229376 | tf_op jit(solution)/shard_map/all_to_all | solution.py:38
  64.4 0.0 copy-start.1
  64.4 0.0 reduce-scatter.4.cloned.1.call-start
  64.5 4.5 %reshape.64 = bf16[4096,1,4]{2,1,0:T(2,128)(2,1)} reshape(bf16[16,2,512]{2,1,0:T(2,128)(2,1)S(1)} %all-to-all-done) | data formatting | bytes 65536
  69.0 4.5 %copy.35 = bf16[4,1,4096]{2,0,1:T(4,128)(2,1)S(1)} copy(bf16[4,1,4096]{0,1,2:T(2,128)(2,1)} %bitcast.103) | data formatting | bytes 65536 | tf_op jit(solution)/shard_map/all_to_all | solution.py:48
  73.5 0.6 reshape.43
  74.2 1.9 %convolution_bitcast_fusion = f32[1024,64]{1,0:T(8,128)} fusion(bf16[64,256]{1,0:T(8,128)(2,1)} %reshape.43, bf16[1,256,1024]{2,1,0:T(8,128)(2,1)S(1)} %copy-done.1), kind=kOutput, calls=%fused_computation.5 | convolution fusion | flops 33554432 | bytes 819200
  76.1 0.0 reduce-scatter.4.cloned.1.call-update
  76.1 0.0 all-to-all-done.1
  76.2 0.5 fusion.1
  76.6 0.0 copy-start.6
  76.6 0.0 copy-start.8
  76.7 64.7 %all-reduce.1 = bf16[64,1024]{1,0:T(8,128)(2,1)S(1)} all-reduce(f32[64,1024]{1,0:T(8,128)S(1)} %fusion.1), channel_id=1, replica_groups=mesh['section'=2,'dp'=16] {'dp'}, use_global_device_ids=true, to_apply=%region_1.0 | all-reduce | flops 65536 | bytes 393216 | tf_op jit(solution)/shard_map/psum | solution.py:65
  141.4 0.0 reduce-scatter.4.cloned.1.call-done
  141.4 0.8 copy.40
  142.2 0.1 convert_select_fusion
  142.3 0.0 copy-done.4
  142.3 0.3 convolution_multiply_fusion
  142.7 3.5 %convolution_bitcast_fusion.1 = f32[4,8]{1,0:T(4,128)S(1)} fusion(bf16[8,64,1024]{2,1,0:T(8,128)(2,1)S(1)} %fusion, f32[4,64,1024]{2,1,0:T(8,128)S(1)} %convolution_multiply_fusion), kind=kOutput, calls=%fused_computation.8 | convolution fusion | flops 25165824 | bytes 2097280 | tf_op jit(solution)/shard_map/mij,qij->mq/dot_general | solution.py:83
  146.2 29.5 %psum.15 = f32[4,8]{1,0:T(4,128)S(1)} all-reduce(f32[4,8]{1,0:T(4,128)S(1)} %convolution_bitcast_fusion.1), channel_id=1, replica_groups=mesh['section'=2,'dp'=16] {'dp'}, use_global_device_ids=true, to_apply=%region_2.3 | all-reduce | flops 32 | bytes 256 | tf_op jit(solution)/shard_map/psum | solution.py:88
  175.7 4.4 %all-gather.1 = f32[2,4,8]{2,1,0:T(4,128)S(1)} all-gather(f32[1,4,8]{2,1,0:T(4,128)S(1)} %bitcast.126), channel_id=2, replica_groups=mesh['section'=2,'dp'=16] {'section'}, dimensions={0}, use_global_device_ids=true | all-gather | bytes 384 | tf_op jit(solution)/shard_map/all_gather | solution.py:11
  180.0 0.8 fusion.3
  (19 shorter events, 0.1 us)
Async XLA Ops:
  6.5 69.6 %copy-start = (bf16[1,896,1024]{2,1,0:T(8,128)(2,1)S(1)}, bf16[1,896,1024]{2,1,0:T(8,128)(2,1)}, u32[]{:S(2)}) copy-start(bf16[1,896,1024]{2,1,0:T(8,128)(2,1)} %param.11) | copy-start | bytes 5505028
  12.0 33.5 %copy-start.7 = (s32[4]{0:T(128)S(1)}, s32[4]{0:T(128)}, u32[]{:S(2)}) copy-start(s32[4]{0:T(128)} %param.15) | copy-start | bytes 52
  12.1 34.1 %copy-start.3 = (bf16[1,4,1,14336]{3,1,2,0:T(4,128)(2,1)S(1)}, bf16[1,4,1,14336]{3,1,2,0:T(4,128)(2,1)}, u32[]{:S(2)}) copy-start(bf16[1,4,1,14336]{3,1,2,0:T(4,128)(2,1)} %param.9) | copy-start | bytes 344068
  12.1 44.2 %copy-start.2 = (f32[1,64,1024]{2,1,0:T(8,128)S(1)}, f32[1,64,1024]{2,1,0:T(8,128)}, u32[]{:S(2)}) copy-start(f32[1,64,1024]{2,1,0:T(8,128)} %param.13) | copy-start | bytes 786436
  38.1 20.3 %all-to-all-start = ((bf16[16,2,512]{2,1,0:T(2,128)(2,1)}), bf16[16,2,512]{2,1,0:T(2,128)(2,1)S(1)}, u32[]{:S(2)}, u32[]{:S(2)}) async-start(bf16[16,2,512]{2,1,0:T(2,128)(2,1)} %reshape.63), calls=%async_computation | async-start | bytes 65536 | tf_op jit(solution)/shard_map/all_to_all | solution.py:48
  58.4 17.7 %all-to-all-start.1 = ((bf16[16,4,1,896]{3,1,2,0:T(4,128)(2,1)}), bf16[16,4,1,896]{3,1,2,0:T(4,128)(2,1)S(1)}, u32[]{:S(2)}, u32[]{:S(2)}) async-start(bf16[16,4,1,896]{3,1,2,0:T(4,128)(2,1)} %constant_dynamic-update-slice_fusion), calls=%async_computation.1 | async-start | bytes 229376 | tf_op jit(solution)/shard_map/all_to_all | solution.py:38
  64.4 9.8 %copy-start.1 = (bf16[1,256,1024]{2,1,0:T(8,128)(2,1)S(1)}, bf16[1,256,1024]{2,1,0:T(8,128)(2,1)}, u32[]{:S(2)}) copy-start(bf16[1,256,1024]{2,1,0:T(8,128)(2,1)} %param.12) | copy-start | bytes 1572868
  64.4 76.9 %reduce-scatter.4.cloned.1.call-start = ((), (), s32[]{:S(2)}) async-start(), calls=%async_computation.3 | async-start | bytes 557056
  74.2 68.0 %copy-start.5 = (pred[64]{0:T(512)(128)(4,1)S(1)}, pred[64]{0:T(512)(128)(4,1)}, u32[]{:S(2)}) copy-start(pred[64]{0:T(512)(128)(4,1)} %lt.31) | copy-start | bytes 196
  74.2 68.1 %copy-start.4 = (f32[4]{0:T(128)S(1)}, f32[4]{0:T(128)}, u32[]{:S(2)}) copy-start(f32[4]{0:T(128)} %convert_divide_fusion.1) | copy-start | bytes 52
  76.6 103.4 %copy-start.6 = (f32[8,8]{1,0:T(8,128)S(1)}, f32[8,8]{1,0:T(8,128)}, u32[]{:S(2)}) copy-start(f32[8,8]{1,0:T(8,128)} %param.17) | copy-start | bytes 772
  76.6 103.4 %copy-start.8 = (s32[4]{0:T(128)S(1)}, s32[4]{0:T(128)}, u32[]{:S(2)}) copy-start(s32[4]{0:T(128)} %param.16) | copy-start | bytes 52
  76.6 103.4 %copy-start.9 = (s32[8]{0:T(128)S(1)}, s32[8]{0:T(128)}, u32[]{:S(2)}) copy-start(s32[8]{0:T(128)} %iota_add_fusion) | copy-start | bytes 100
Sparse Core Ops, SparseCore 0:
  76.2 57.6 reduce-scatter.3
